TPU v7x, 8 devices: a whole 2x2x1 slice. The times are simulated.
8 devices in a mesh: inst: 1 (over z), dev: 2 (over y), side: 4 (over x, core).
Axes of the slice: x: 2, y: 2, z: 1, core: 2. Of those that a mesh axis runs over, the one named last changes fastest.
Arguments:
- hidden: bfloat16 [512, 3584], P(('inst', 'dev'))
- cache_len: int32 [512], P(('inst', 'dev'))
- k_cache: bfloat16 [3, 512, 4, 64, 128], P(None, ('inst', 'dev'))
- v_cache: bfloat16 [3, 512, 4, 64, 128], P(None, ('inst', 'dev'))
- w_q: bfloat16 [3, 3584, 3584], replicated
- w_kv: bfloat16 [3, 3584, 1024], replicated
- w_o: bfloat16 [3, 3584, 3584], replicated
- attn_gain: float32 [3, 3584], replicated
- ffn_gain: float32 [3, 3584], replicated
- w_gate: bfloat16 [3, 3584, 18944], P(None, None, 'dev')
- w_up: bfloat16 [3, 3584, 18944], P(None, None, 'dev')
- w_down: bfloat16 [3, 18944, 3584], P(None, 'dev')
Outputs:
- output: bfloat16 [512, 3584], P(('inst', 'dev', 'side'))
All inputs are finite; a program needn't handle non-finite values.
Results may differ from a plain program's by a relative error of at most 0.02.
Values are sent between devices in bfloat16 or wider.
A program may use at most 3.5 GiB of HBM per device.

v0:
```python
import jax
import jax.numpy as jnp
from jax import lax
from jax.sharding import PartitionSpec as P

EPS = 1e-5
ROPE_BASE = 10000.0


def rms_norm(rows, gain):
    rows_f = rows.astype(jnp.float32)
    inv_rms = lax.rsqrt(jnp.mean(rows_f * rows_f, axis=-1, keepdims=True) + EPS)
    return (rows_f * inv_rms * gain).astype(jnp.bfloat16)


def rotary(vecs, positions):
    half_dim = vecs.shape[-1] // 2
    freqs = ROPE_BASE ** (-jnp.arange(half_dim, dtype=jnp.float32) / half_dim)
    angle = positions.astype(jnp.float32)[:, None, None] * freqs
    cos_part = jnp.cos(angle)
    sin_part = jnp.sin(angle)
    first = vecs[..., :half_dim]
    second = vecs[..., half_dim:]
    return jnp.concatenate([first * cos_part - second * sin_part, second * cos_part + first * sin_part], axis=-1)


def attention_layer(x_rows, lengths, k_seq, v_seq, q_weight, kv_weight, o_weight, gain_attn):
    count = x_rows.shape[0]
    kv_heads = k_seq.shape[1]
    head_dim = k_seq.shape[-1]
    normed = rms_norm(x_rows, gain_attn)
    q_all = jnp.dot(normed, q_weight, preferred_element_type=jnp.float32).reshape(count, -1, head_dim)
    kv_all = jnp.dot(normed, kv_weight, preferred_element_type=jnp.float32).reshape(count, 2, kv_heads, head_dim)
    q_rows = rotary(q_all, lengths).astype(jnp.bfloat16).reshape(count, kv_heads, -1, head_dim)
    k_new = rotary(kv_all[:, 0], lengths).astype(jnp.bfloat16)
    v_new = kv_all[:, 1].astype(jnp.bfloat16)
    scale = head_dim ** -0.5
    scores = jnp.einsum('nkgd,nksd->nkgs', q_rows, k_seq, preferred_element_type=jnp.float32) * scale
    valid = jnp.arange(k_seq.shape[2])[None, None, None, :] < lengths[:, None, None, None]
    scores = jnp.where(valid, scores, -1e30)
    self_score = jnp.einsum('nkgd,nkd->nkg', q_rows, k_new, preferred_element_type=jnp.float32) * scale
    row_max = jnp.maximum(jnp.max(scores, axis=-1), self_score)
    exp_scores = jnp.exp(scores - row_max[..., None])
    self_exp = jnp.exp(self_score - row_max)
    total_exp = jnp.sum(exp_scores, axis=-1) + self_exp
    mixed = jnp.einsum('nkgs,nksd->nkgd', exp_scores.astype(jnp.bfloat16), v_seq, preferred_element_type=jnp.float32)
    mixed = mixed + self_exp.astype(jnp.bfloat16).astype(jnp.float32)[..., None] * v_new.astype(jnp.float32)[:, :, None, :]
    mixed = (mixed / total_exp[..., None]).astype(jnp.bfloat16).reshape(count, -1)
    attn_out = jnp.dot(mixed, o_weight, preferred_element_type=jnp.float32)
    return (x_rows.astype(jnp.float32) + attn_out).astype(jnp.bfloat16)


def ffn_partial(h_rows, gate_weight, up_weight, down_weight):
    gate = jnp.dot(h_rows, gate_weight, preferred_element_type=jnp.float32)
    up_proj = jnp.dot(h_rows, up_weight, preferred_element_type=jnp.float32)
    act_rows = (jax.nn.silu(gate) * up_proj).astype(jnp.bfloat16)
    return jnp.dot(act_rows, down_weight, preferred_element_type=jnp.float32)


def pair_rows(local, slot, half_side):
    shaped = local.reshape((2, half_side, local.shape[0] // (2 * half_side)) + local.shape[1:])
    picked = lax.dynamic_index_in_dim(shaped, slot, axis=1, keepdims=False)
    return picked.reshape((-1,) + local.shape[1:])


def keep_rows(x_in):
    return x_in


def skip_ffn(h_in):
    return jnp.zeros(h_in.shape, jnp.float32)


def solution(mesh):
    n_side = mesh.shape['side']
    half_side = n_side // 2
    to_ffn = [(slot, slot + half_side) for slot in range(half_side)]
    to_attn = [(slot + half_side, slot) for slot in range(half_side)]
    batch_axes = ('inst', 'dev')
    in_specs = (
        P(batch_axes, None),
        P(batch_axes),
        P(None, batch_axes, None, None, None),
        P(None, batch_axes, None, None, None),
        P(), P(), P(), P(), P(),
        P(None, None, 'dev'),
        P(None, None, 'dev'),
        P(None, 'dev', None),
    )
    out_specs = P(('inst', 'dev', 'side'), None)

    def device_fn(hidden, cache_len, k_cache, v_cache, w_q, w_kv, w_o, attn_gain, ffn_gain, w_gate, w_up, w_down):
        side_idx = lax.axis_index('side')
        is_attn = side_idx < half_side
        slot = side_idx % half_side
        rows = hidden.shape[0] // n_side
        n_layers = w_q.shape[0]
        x_pair = pair_rows(hidden, slot, half_side)
        lengths = pair_rows(cache_len, slot, half_side)
        for layer in range(n_layers):
            def attn_branch(x_in, layer=layer):
                k_seq = pair_rows(k_cache[layer], slot, half_side)
                v_seq = pair_rows(v_cache[layer], slot, half_side)
                return attention_layer(x_in, lengths, k_seq, v_seq, w_q[layer], w_kv[layer], w_o[layer], attn_gain[layer])

            def ffn_branch(h_in, layer=layer):
                return ffn_partial(h_in, w_gate[layer], w_up[layer], w_down[layer])

            x_pair = lax.cond(is_attn, attn_branch, keep_rows, x_pair)
            sent = lax.ppermute(x_pair, 'side', to_ffn)
            h_rows = rms_norm(sent, ffn_gain[layer])
            h_all = lax.all_gather(h_rows, 'dev', axis=0, tiled=True)
            part_sum = lax.cond(is_attn, skip_ffn, ffn_branch, h_all)
            summed = lax.psum_scatter(part_sum, 'dev', scatter_dimension=0, tiled=True)
            x_ffn = (sent.astype(jnp.float32) + summed.astype(jnp.bfloat16).astype(jnp.float32)).astype(jnp.bfloat16)
            if layer + 1 < n_layers:
                x_pair = lax.ppermute(x_ffn, 'side', to_attn)
            else:
                back = lax.ppermute(x_ffn[:rows], 'side', to_attn)
                out_rows = jnp.where(is_attn, back, x_ffn[rows:])
        return out_rows

    return jax.shard_map(device_fn, mesh=mesh, in_specs=in_specs, out_specs=out_specs, check_vma=False)
```

profile of v0, /device:TPU:0, one launch (start us, length us, event | category | flops | bytes accessed | tf_op | source)
XLA Modules:
  0.0 1345.8 jit_solution(17020260384795510785)
XLA Ops:
  10.5 231.0 %conditional.6 = (bf16[128,3584]{1,0:T(8,128)(2,1)S(1)}) conditional(s32[]{:T(128)} %convert_element_type.200, bf16[128,3584]{1,0:T(8,128)(2,1)S(1)} %bitcast.267, (bf16[128,3584]{1,0:T(8,128)(2,1)S(1)}, s32[2,64]{1,0:T(2,128)}, f32[3,3584]{1,0:T(4,128)}, bf16[3,3584,3584]{2,1,0:T(8,128)(2,1)}, s32[128]{0:T(128)}, ...), branch_computations={%region_0.1_spmd, %region_1.5_spmd} | conditional | flops 7651464704 | bytes 474995008 | solution.py:109
  11.6 28.6 %copy.55 = bf16[3,3584,1024]{1,2,0:T(8,128)(2,1)} copy(bf16[3,3584,1024]{2,1,0:T(8,128)(2,1)} %get-tuple-element.189) | data formatting | bytes 44040192 | tf_op jit(solution)/shard_map
  46.6 89.6 %copy.54 = bf16[3,3584,3584]{1,2,0:T(8,128)(2,1)} copy(bf16[3,3584,3584]{2,1,0:T(8,128)(2,1)} %get-tuple-element.185) | data formatting | bytes 154140672 | tf_op jit(solution)/shard_map
  136.2 20.8 %slice.158 = bf16[1,3584,3584]{1,2,0:T(8,128)(2,1)} slice(bf16[3,3584,3584]{1,2,0:T(8,128)(2,1)} %copy.54), slice={[0:1], [0:3584], [0:3584]} | slice | bytes 51380224 | tf_op jit(solution)/shard_map/cond/branch_1_fun/slice | solution.py:104
  157.0 11.9 fusion.88
  172.6 3.4 copy.36
  178.0 8.4 slice.112
  186.4 14.2 %slice.107 = bf16[1,256,4,64,128]{4,3,2,1,0:T(8,128)(2,1)} slice(bf16[3,256,4,64,128]{4,3,2,1,0:T(8,128)(2,1)} %get-tuple-element.115), slice={[0:1], [0:256], [0:4], [0:64], [0:128]} | slice | bytes 33554432 | tf_op jit(solution)/shard_map/cond/branch_1_fun/slice | solution.py:102
  200.6 11.7 constant_dynamic-slice_fusion
  212.5 8.4 fusion.75
  223.5 5.4 divide_convert_fusion
  230.5 10.5 fusion.72
  244.5 18.8 %collective-permute-done = bf16[128,3584]{1,0:T(8,128)(2,1)S(1)} collective-permute-done((bf16[128,3584]{1,0:T(8,128)(2,1)S(1)}, bf16[128,3584]{1,0:T(8,128)(2,1)S(1)}, u32[]{:S(2)}, u32[]{:S(2)}) %collective-permute-start) | collective-permute-done | bytes 917536 | tf_op jit(solution)/shard_map/ppermute | solution.py:110
  264.9 30.4 %all-gather.4.cloned.1.call-done = bf16[256,3584]{1,0:T(8,128)(2,1)} async-done(((bf16[128,3584]{1,0:T(8,128)(2,1)}), bf16[256,3584]{1,0:T(8,128)(2,1)}) %all-gather.4.cloned.1.call-update) | async-done | bytes 1835024 | tf_op jit(solution)/shard_map/all_gather | solution.py:112
  297.6 136.0 %reduce-scatter.4.cloned.1.call-done = f32[128,3584]{1,0:T(8,128)} async-done(((f32[256,3584]{1,0:T(8,128)}), f32[128,3584]{1,0:T(8,128)}) %reduce-scatter.4.cloned.1.call-update) | async-done | bytes 1835024 | tf_op jit(solution)/shard_map/reduce_scatter | solution.py:114
  436.6 22.4 %collective-permute-done.1 = bf16[128,3584]{1,0:T(8,128)(2,1)} collective-permute-done((bf16[128,3584]{1,0:T(8,128)(2,1)S(1)}, bf16[128,3584]{1,0:T(8,128)(2,1)}, u32[]{:S(2)}, u32[]{:S(2)}) %collective-permute-start.1) | collective-permute-done | bytes 917536 | tf_op jit(solution)/shard_map/ppermute | solution.py:117
  459.0 228.4 %conditional.8 = (bf16[128,3584]{1,0:T(8,128)(2,1)}) conditional(s32[]{:T(128)} %convert_element_type.200, bf16[128,3584]{1,0:T(8,128)(2,1)} %collective-permute-done.1, (bf16[128,3584]{1,0:T(8,128)(2,1)}, s32[2,64]{1,0:T(2,128)S(1)}, f32[3,3584]{1,0:T(4,128)S(1)}, bf16[3,3584,3584]{2,1,0:T(8,128)(2,1)}, s32[128]{0:T(128)}, ...), branch_computations={%region_9.10_spmd, %region_10.14_spmd} | conditional | flops 7651464704 | bytes 474988672 | solution.py:109
  460.7 28.6 %copy.57 = bf16[3,3584,1024]{1,2,0:T(8,128)(2,1)} copy(bf16[3,3584,1024]{2,1,0:T(8,128)(2,1)} %get-tuple-element.199) | data formatting | bytes 44040192 | tf_op jit(solution)/shard_map
  492.4 3.3 fusion.121
  497.6 89.6 %copy.56 = bf16[3,3584,3584]{1,2,0:T(8,128)(2,1)} copy(bf16[3,3584,3584]{2,1,0:T(8,128)(2,1)} %get-tuple-element.195) | data formatting | bytes 154140672 | tf_op jit(solution)/shard_map
  587.1 20.8 %slice.166 = bf16[1,3584,3584]{1,2,0:T(8,128)(2,1)} slice(bf16[3,3584,3584]{1,2,0:T(8,128)(2,1)} %copy.56), slice={[1:2], [0:3584], [0:3584]} | slice | bytes 51380224 | tf_op jit(solution)/shard_map/cond/branch_1_fun/slice | solution.py:104
  607.9 12.2 fusion.123
  626.1 8.4 slice.122
  634.5 14.2 %slice.127 = bf16[1,256,4,64,128]{4,3,2,1,0:T(8,128)(2,1)} slice(bf16[3,256,4,64,128]{4,3,2,1,0:T(8,128)(2,1)} %get-tuple-element.132), slice={[1:2], [0:256], [0:4], [0:64], [0:128]} | slice | bytes 33554432 | tf_op jit(solution)/shard_map/cond/branch_1_fun/slice | solution.py:103
  648.6 11.5 constant_dynamic-slice_fusion.2
  660.3 7.1 fusion.110
  669.3 5.4 divide_convert_fusion.1
  675.7 11.4 fusion.107
  688.8 18.8 %collective-permute-done.2 = bf16[128,3584]{1,0:T(8,128)(2,1)S(1)} collective-permute-done((bf16[128,3584]{1,0:T(8,128)(2,1)}, bf16[128,3584]{1,0:T(8,128)(2,1)S(1)}, u32[]{:S(2)}, u32[]{:S(2)}) %collective-permute-start.2) | collective-permute-done | bytes 917536 | tf_op jit(solution)/shard_map/ppermute | solution.py:110
  709.1 28.6 %all-gather.6.cloned.1.call-done = bf16[256,3584]{1,0:T(8,128)(2,1)} async-done(((bf16[128,3584]{1,0:T(8,128)(2,1)}), bf16[256,3584]{1,0:T(8,128)(2,1)}) %all-gather.6.cloned.1.call-update) | async-done | bytes 1835024 | tf_op jit(solution)/shard_map/all_gather | solution.py:112
  740.0 135.8 %reduce-scatter.6.cloned.1.call-done = f32[128,3584]{1,0:T(8,128)} async-done(((f32[256,3584]{1,0:T(8,128)}), f32[128,3584]{1,0:T(8,128)}) %reduce-scatter.6.cloned.1.call-update) | async-done | bytes 1835024 | tf_op jit(solution)/shard_map/reduce_scatter | solution.py:114
  878.7 22.4 %collective-permute-done.3 = bf16[128,3584]{1,0:T(8,128)(2,1)} collective-permute-done((bf16[128,3584]{1,0:T(8,128)(2,1)S(1)}, bf16[128,3584]{1,0:T(8,128)(2,1)}, u32[]{:S(2)}, u32[]{:S(2)}) %collective-permute-start.3) | collective-permute-done | bytes 917536 | tf_op jit(solution)/shard_map/ppermute | solution.py:117
  901.2 228.2 %conditional.10 = (bf16[128,3584]{1,0:T(8,128)(2,1)}) conditional(s32[]{:T(128)} %convert_element_type.200, bf16[128,3584]{1,0:T(8,128)(2,1)} %collective-permute-done.3, (bf16[128,3584]{1,0:T(8,128)(2,1)}, s32[2,64]{1,0:T(2,128)S(1)}, f32[3,3584]{1,0:T(4,128)S(1)}, bf16[3,3584,3584]{2,1,0:T(8,128)(2,1)}, s32[128]{0:T(128)}, ...), branch_computations={%region_18.19_spmd, %region_19.23_spmd} | conditional | flops 7651464704 | bytes 474988672 | solution.py:109
  902.7 28.8 %copy.59 = bf16[3,3584,1024]{1,2,0:T(8,128)(2,1)} copy(bf16[3,3584,1024]{2,1,0:T(8,128)(2,1)} %get-tuple-element.209) | data formatting | bytes 44040192 | tf_op jit(solution)/shard_map
  934.5 3.3 fusion.156
  939.7 89.6 %copy.58 = bf16[3,3584,3584]{1,2,0:T(8,128)(2,1)} copy(bf16[3,3584,3584]{2,1,0:T(8,128)(2,1)} %get-tuple-element.205) | data formatting | bytes 154140672 | tf_op jit(solution)/shard_map
  1029.3 20.8 %slice.174 = bf16[1,3584,3584]{1,2,0:T(8,128)(2,1)} slice(bf16[3,3584,3584]{1,2,0:T(8,128)(2,1)} %copy.58), slice={[2:3], [0:3584], [0:3584]} | slice | bytes 51380224 | tf_op jit(solution)/shard_map/cond/branch_1_fun/slice | solution.py:104
  1050.0 12.2 fusion.158
  1068.2 8.4 slice.137
  1076.6 14.2 %slice.142 = bf16[1,256,4,64,128]{4,3,2,1,0:T(8,128)(2,1)} slice(bf16[3,256,4,64,128]{4,3,2,1,0:T(8,128)(2,1)} %get-tuple-element.146), slice={[2:3], [0:256], [0:4], [0:64], [0:128]} | slice | bytes 33554432 | tf_op jit(solution)/shard_map/cond/branch_1_fun/slice | solution.py:103
  1090.8 11.5 constant_dynamic-slice_fusion.4
  1102.4 7.1 fusion.145
  1111.4 5.4 divide_convert_fusion.2
  1117.8 11.4 fusion.142
  1130.7 18.8 %collective-permute-done.4 = bf16[128,3584]{1,0:T(8,128)(2,1)S(1)} collective-permute-done((bf16[128,3584]{1,0:T(8,128)(2,1)}, bf16[128,3584]{1,0:T(8,128)(2,1)S(1)}, u32[]{:S(2)}, u32[]{:S(2)}) %collective-permute-start.4) | collective-permute-done | bytes 917536 | tf_op jit(solution)/shard_map/ppermute | solution.py:110
  1151.0 28.6 %all-gather.8.cloned.1.call-done = bf16[256,3584]{1,0:T(8,128)(2,1)} async-done(((bf16[128,3584]{1,0:T(8,128)(2,1)}), bf16[256,3584]{1,0:T(8,128)(2,1)}) %all-gather.8.cloned.1.call-update) | async-done | bytes 1835024 | tf_op jit(solution)/shard_map/all_gather | solution.py:112
  1181.9 140.2 %reduce-scatter.8.cloned.1.call-done = f32[128,3584]{1,0:T(8,128)} async-done(((f32[256,3584]{1,0:T(8,128)}), f32[128,3584]{1,0:T(8,128)}) %reduce-scatter.8.cloned.1.call-update) | async-done | bytes 1835024 | tf_op jit(solution)/shard_map/reduce_scatter | solution.py:114
  1325.1 12.6 collective-permute-done.5
  (152 shorter events, 85.6 us)
Async XLA Ops:
  6.5 1.5 copy-start
  6.5 288.7 %all-gather.4.cloned.1.call-start = ((), (), s32[]{:S(2)}) async-start(), calls=%async_computation.3 | async-start | bytes 2752512 | tf_op jit(solution)/shard_map/all_gather | solution.py:112
  10.8 29.5 %copy-start.14 = (f32[128]{0:T(128)}, f32[128]{0:T(128)S(1)}, u32[]{:S(2)}) copy-start(f32[128]{0:T(128)S(1)} %add_rsqrt_fusion) | copy-start | bytes 1540 | tf_op jit(solution)/shard_map/cond
  40.2 3.1 slice-start
  46.3 89.9 %copy-start.7 = (f32[128,64]{0,1:T(8,128)}, f32[128,64]{0,1:T(8,128)S(1)}, u32[]{:S(2)}) copy-start(f32[128,64]{0,1:T(8,128)S(1)} %get-tuple-element.223) | copy-start | bytes 98308 | tf_op jit(solution)/shard_map/cond
  46.3 89.9 %copy-start.9 = (f32[128,64]{0,1:T(8,128)}, f32[128,64]{0,1:T(8,128)S(1)}, u32[]{:S(2)}) copy-start(f32[128,64]{0,1:T(8,128)S(1)} %get-tuple-element.224) | copy-start | bytes 98308 | tf_op jit(solution)/shard_map/cond
  136.2 20.8 %copy-start.15 = (f32[128]{0:T(128)S(1)}, f32[128]{0:T(128)}, u32[]{:S(2)}) copy-start(f32[128]{0:T(128)} %copy-done.14) | copy-start | bytes 1540 | tf_op jit(solution)/shard_map/cond
  157.0 11.9 copy-start.8
  157.0 12.0 copy-start.10
  200.6 11.7 copy-start.17
  220.9 2.4 copy-start.2
  241.5 21.8 %collective-permute-start = (bf16[128,3584]{1,0:T(8,128)(2,1)S(1)}, bf16[128,3584]{1,0:T(8,128)(2,1)S(1)}, u32[]{:S(2)}, u32[]{:S(2)}) collective-permute-start(bf16[128,3584]{1,0:T(8,128)(2,1)S(1)} %get-tuple-element.253), channel_id=1, source_target_pairs={{0,2},{1,3},{4,6},{5,7}} | collective-permute-start | bytes 2752520 | tf_op jit(solution)/shard_map/ppermute | solution.py:110
  264.8 168.8 %reduce-scatter.4.cloned.1.call-start = ((), (), s32[]{:S(2)}) async-start(), calls=%async_computation.4 | async-start | bytes 5505024 | tf_op jit(solution)/shard_map/reduce_scatter | solution.py:114
  297.5 161.5 %copy-start.13 = (f32[3,3584]{1,0:T(4,128)S(1)}, f32[3,3584]{1,0:T(4,128)}, u32[]{:S(2)}) copy-start(f32[3,3584]{1,0:T(4,128)} %param.31) | copy-start | bytes 129028
  297.5 161.5 %copy-start.16 = (s32[2,1,64]{2,1,0:T(1,128)S(1)}, s32[2,1,64]{2,1,0:T(1,128)}, u32[]{:S(2)}) copy-start(s32[2,1,64]{2,1,0:T(1,128)} %get-tuple-element.216) | copy-start | bytes 1540
  297.5 440.1 %all-gather.6.cloned.1.call-start = ((), (), s32[]{:S(2)}) async-start(), calls=%async_computation.5 | async-start | bytes 2752512 | tf_op jit(solution)/shard_map/all_gather | solution.py:112
  435.3 23.7 %collective-permute-start.1 = (bf16[128,3584]{1,0:T(8,128)(2,1)S(1)}, bf16[128,3584]{1,0:T(8,128)(2,1)}, u32[]{:S(2)}, u32[]{:S(2)}) collective-permute-start(bf16[128,3584]{1,0:T(8,128)(2,1)S(1)} %fusion.174), channel_id=1, source_target_pairs={{2,0},{3,1},{6,4},{7,5}} | collective-permute-start | bytes 2752520 | tf_op jit(solution)/shard_map/ppermute | solution.py:117
  459.0 248.8 %copy-start.12 = (f32[3584]{0:T(1024)S(1)}, f32[3584]{0:T(1024)}, u32[]{:S(2)}) copy-start(f32[3584]{0:T(1024)} %get-tuple-element.214) | copy-start | bytes 43012
  489.3 3.1 slice-start.1
  621.1 4.1 copy-start.5
  667.4 1.7 copy-start.3
  687.4 20.1 %collective-permute-start.2 = (bf16[128,3584]{1,0:T(8,128)(2,1)}, bf16[128,3584]{1,0:T(8,128)(2,1)S(1)}, u32[]{:S(2)}, u32[]{:S(2)}) collective-permute-start(bf16[128,3584]{1,0:T(8,128)(2,1)} %get-tuple-element.255), channel_id=1, source_target_pairs={{0,2},{1,3},{4,6},{5,7}} | collective-permute-start | bytes 2752520 | tf_op jit(solution)/shard_map/ppermute | solution.py:110
  709.1 166.7 %reduce-scatter.6.cloned.1.call-start = ((), (), s32[]{:S(2)}) async-start(), calls=%async_computation.6 | async-start | bytes 5505024 | tf_op jit(solution)/shard_map/reduce_scatter | solution.py:114
  739.9 439.7 %all-gather.8.cloned.1.call-start = ((), (), s32[]{:S(2)}) async-start(), calls=%async_computation.7 | async-start | bytes 2752512 | tf_op jit(solution)/shard_map/all_gather | solution.py:112
  877.4 23.7 %collective-permute-start.3 = (bf16[128,3584]{1,0:T(8,128)(2,1)S(1)}, bf16[128,3584]{1,0:T(8,128)(2,1)}, u32[]{:S(2)}, u32[]{:S(2)}) collective-permute-start(bf16[128,3584]{1,0:T(8,128)(2,1)S(1)} %fusion.178), channel_id=1, source_target_pairs={{2,0},{3,1},{6,4},{7,5}} | collective-permute-start | bytes 2752520 | tf_op jit(solution)/shard_map/ppermute | solution.py:117
  901.2 248.6 %copy-start.11 = (f32[3584]{0:T(1024)S(1)}, f32[3584]{0:T(1024)}, u32[]{:S(2)}) copy-start(f32[3584]{0:T(1024)} %get-tuple-element.212) | copy-start | bytes 43012
  931.4 3.1 slice-start.2
  1063.3 4.1 copy-start.6
  1109.5 1.7 copy-start.4
  1129.3 20.1 %collective-permute-start.4 = (bf16[128,3584]{1,0:T(8,128)(2,1)}, bf16[128,3584]{1,0:T(8,128)(2,1)S(1)}, u32[]{:S(2)}, u32[]{:S(2)}) collective-permute-start(bf16[128,3584]{1,0:T(8,128)(2,1)} %get-tuple-element.257), channel_id=1, source_target_pairs={{0,2},{1,3},{4,6},{5,7}} | collective-permute-start | bytes 2752520 | tf_op jit(solution)/shard_map/ppermute | solution.py:110
  1151.0 171.1 %reduce-scatter.8.cloned.1.call-start = ((), (), s32[]{:S(2)}) async-start(), calls=%async_computation.8 | async-start | bytes 5505024 | tf_op jit(solution)/shard_map/reduce_scatter | solution.py:114
  1181.9 156.7 %copy-start.1 = (bf16[256,3584]{1,0:T(8,128)(2,1)S(1)}, bf16[256,3584]{1,0:T(8,128)(2,1)}, u32[]{:S(2)}) copy-start(bf16[256,3584]{1,0:T(8,128)(2,1)} %param.24) | copy-start | bytes 5505028
  1323.8 13.9 %collective-permute-start.5 = (bf16[64,3584]{1,0:T(8,128)(2,1)S(1)}, bf16[64,3584]{1,0:T(8,128)(2,1)S(1)}, u32[]{:S(2)}, u32[]{:S(2)}) collective-permute-start(bf16[64,3584]{1,0:T(8,128)(2,1)S(1)} %slice.182), channel_id=1, source_target_pairs={{2,0},{3,1},{6,4},{7,5}} | collective-permute-start | bytes 1376264 | tf_op jit(solution)/shard_map/ppermute | solution.py:119
Sparse Core Ops, SparseCore 0:
  264.9 30.2 all-gather.3
  297.6 135.9 reduce-scatter.3
  709.2 28.4 all-gather.5
  740.0 135.6 reduce-scatter.5
  1151.1 28.4 all-gather.7
  1182.0 140.0 reduce-scatter.7
where the time goes:
time: 1360 us; the launch traced here: 1350 us
  waiting for transfers between devices  614 us (45%)
  local copies, waits for them, and re-layouts  562 us (41%)
  matrix products  121 us (9%)
  other arithmetic  25.6 us (2%)
  between operations  14 us (1%)
    reduce_scatter x3, waiting for transfers between devices, device_fn(): summed = lax.psum_scatter(part_sum, 'dev', scatter_dimension=0, tiled=True)  412 us
    another operation x9, local copies, waits for them, and re-layouts  361 us
    all_gather x3, waiting for transfers between devices, device_fn(): h_all = lax.all_gather(h_rows, 'dev', axis=0, tiled=True)  87.5 us
    slice x3, local copies, waits for them, and re-layouts, attn_branch(): w_q[layer]  62.4 us
    ppermute x3, waiting for transfers between devices, device_fn(): sent = lax.ppermute(x_pair, 'side', to_ffn)  56.4 us
    ppermute x2, waiting for transfers between devices, device_fn(): x_pair = lax.ppermute(x_ffn, 'side', to_attn)  44.9 us
    slice x3, local copies, waits for them, and re-layouts, attn_branch(): v_seq = pair_rows(v_cache[layer], slot, half_side)  36.7 us
    dynamic_slice x6, local copies, waits for them, and re-layouts, pair_rows(): picked = lax.dynamic_index_in_dim(shaped, slot, axis=1, keepdims=False)  36.4 us
  transfers between devices with their start and end apart: 12, of which 12 were waited for; matrix products, arithmetic and copies ran while one was open for 0% of the time, Pallas kernels for 0%

commit v1 on v0

v1 whole, which is shorter than its diff:
```python
import functools

import jax
import jax.numpy as jnp
from jax import lax
from jax.experimental import pallas as pl
from jax.experimental.pallas import tpu as pltpu
from jax.sharding import PartitionSpec as P

EPS = 1e-5
ROPE_BASE = 10000.0
MESH = pl.DeviceIdType.MESH
F32 = jnp.float32
BF16 = jnp.bfloat16

TN = 256
NS = 16
GS = 8
CS = 32
GU_UNROLL = 4
DN_UNROLL = 2


def dot(lhs, rhs):
    return jnp.dot(lhs, rhs, preferred_element_type=F32)


def kernel(dims, cos_ref, sin_ref, len_ref, ag_ref, fg_ref, hid, kc, vc, wq, wkv, wo, wg, wu, wd, out,
           ring, xc, x1, h, qf, kn, vn, of, oa, u, yp, dr, yr, kb, vb,
           ring_sem, cache_sem, in_sem, o_send, o_recv, xp_send, xp_recv, xy_send, xy_recv, xf_send, xf_recv,
           d_send, d_recv, y_send, y_recv, e_send, e_recv):
    n_layers, d_model, ff, heads, kv_heads, head, seq = dims
    half_d = d_model // 2
    nch = d_model // TN
    nq = half_d // TN
    rows = xc.shape[2]
    ngu = ff // 128
    group = heads // kv_heads
    r_kv = nq
    r_o = nq + 2
    r_gu = r_o + nq
    r_dn = r_gu + ngu
    tiles = r_dn + nch

    side = lax.axis_index("side")
    dev = lax.axis_index("dev")
    c = lax.rem(side, 2)
    oc = 1 - c
    base = (side - c) * rows
    pair = {"side": side + 1 - 2 * c}
    ypeer = {"dev": 1 - dev}

    barrier = pltpu.get_barrier_semaphore()
    pl.semaphore_signal(barrier, inc=1, device_id=pair, device_id_type=MESH)
    pl.semaphore_signal(barrier, inc=1, device_id=ypeer, device_id_type=MESH)

    def rcopy(src, dst, ssem, rsem, where):
        return pltpu.make_async_remote_copy(
            src_ref=src, dst_ref=dst, send_sem=ssem, recv_sem=rsem, device_id=where, device_id_type=MESH)

    def al(v, m):
        return pl.multiple_of(v, m)

    def slot_of(layer, r):
        return lax.rem(layer * tiles + r, NS)

    def issue(layer, r):
        slot = slot_of(layer, r)
        sem = ring_sem.at[slot]
        top = ring.at[slot, pl.ds(0, d_model)]

        @pl.when(r < r_kv)
        def _():
            pltpu.make_async_copy(wq.at[layer, :, pl.ds(al(c * half_d + r * TN, TN), TN)], top, sem).start()

        @pl.when((r >= r_kv) & (r < r_o))
        def _():
            col = (r - r_kv) * (2 * TN) + c * TN
            pltpu.make_async_copy(wkv.at[layer, :, pl.ds(al(col, TN), TN)], top, sem).start()

        @pl.when((r >= r_o) & (r < r_gu))
        def _():
            col = c * half_d + (r - r_o) * TN
            pltpu.make_async_copy(wo.at[layer, :, pl.ds(al(col, TN), TN)], top, sem).start()

        @pl.when((r >= r_gu) & (r < r_dn))
        def _():
            col = al(c * ff + (r - r_gu) * 128, 128)
            pltpu.make_async_copy(
                wg.at[layer, :, pl.ds(col, 128)], ring.at[slot, pl.ds(0, d_model), pl.ds(0, 128)], sem).start()
            pltpu.make_async_copy(
                wu.at[layer, :, pl.ds(col, 128)], ring.at[slot, pl.ds(0, d_model), pl.ds(128, 128)], sem).start()

        @pl.when(r >= r_dn)
        def _():
            pltpu.make_async_copy(
                wd.at[layer, pl.ds(al(c * ff, 128), ff), pl.ds(al((r - r_dn) * TN, TN), TN)], ring.at[slot], sem).start()

    def release(layer, r):
        nxt = r + NS
        wrap = (nxt >= tiles).astype(jnp.int32) if not isinstance(nxt, int) else int(nxt >= tiles)
        lay = layer + wrap
        rr = nxt - tiles * wrap

        @pl.when(lay < n_layers)
        def _():
            issue(lay, rr)

    def wait_top(layer, r):
        slot = slot_of(layer, r)
        pltpu.make_async_copy(wq.at[0, :, pl.ds(0, TN)], ring.at[slot, pl.ds(0, d_model)], ring_sem.at[slot]).wait()
        return slot

    def wait_full(layer, r):
        slot = slot_of(layer, r)
        pltpu.make_async_copy(wd.at[0, pl.ds(0, ff), pl.ds(0, TN)], ring.at[slot], ring_sem.at[slot]).wait()
        return slot

    def cache_copies(layer, ch):
        slot = ch % 2 if isinstance(ch, int) else lax.rem(ch, 2)
        src = pl.ds(al(base + ch * CS, CS), CS)
        hd = pl.ds(c * 2, 2)
        return (pltpu.make_async_copy(kc.at[layer, src, hd], kb.at[slot], cache_sem.at[slot, 0]),
                pltpu.make_async_copy(vc.at[layer, src, hd], vb.at[slot], cache_sem.at[slot, 1]))

    def norm_rows(src, chip, gain, layer, dst_row):
        for k in range(2):
            for part in range(rows // 32):
                rs = slice(part * 32, part * 32 + 32)
                total = jnp.zeros((32, TN), F32)
                for j in range(nch):
                    v = (src[chip, j, k, rs, :] if chip is not None else src[j, k, rs, :]).astype(F32)
                    total = total + v * v
                inv = lax.rsqrt(jnp.sum(total, axis=-1, keepdims=True) * (1.0 / d_model) + EPS)
                r0 = dst_row + k * rows + part * 32
                for j in range(nch):
                    v = (src[chip, j, k, rs, :] if chip is not None else src[j, k, rs, :]).astype(F32)
                    h[r0:r0 + 32, j * TN:(j + 1) * TN] = (v * inv * gain[layer, j]).astype(BF16)

    for r in range(NS):
        issue(0, jnp.int32(r))
    for ch in range(2):
        for cp in cache_copies(0, ch):
            cp.start()
    for j in range(nch):
        for k in range(2):
            pltpu.make_async_copy(
                hid.at[pl.ds(al(base + k * rows, rows), rows), pl.ds(j * TN, TN)], xc.at[j, k], in_sem.at[j, k]).start()
    for j in range(nch):
        for k in range(2):
            pltpu.make_async_copy(hid.at[pl.ds(0, rows), pl.ds(0, TN)], xc.at[j, k], in_sem.at[j, k]).wait()
    pl.semaphore_wait(barrier, 2)

    col = lax.broadcasted_iota(jnp.int32, (GS, GS * seq), 1)
    row = lax.broadcasted_iota(jnp.int32, (GS, GS * seq), 0)
    own_keys = lax.shift_right_logical(col, seq.bit_length() - 1) == row
    key_pos = jnp.bitwise_and(col, seq - 1)
    scale = head ** -0.5

    def layer_body(layer, carry):
        not_last = layer + 1 < n_layers

        norm_rows(xc, None, ag_ref, layer, 0)
        cos_v = cos_ref[...]
        sin_v = sin_ref[...]

        def rope(v):
            return (v * cos_v + pltpu.roll(v, head // 2, 1) * sin_v).astype(BF16).astype(F32)

        for g0 in range(0, r_o, 3):
            rs = list(range(g0, min(g0 + 3, r_o)))
            slots = [wait_top(layer, r) for r in rs]
            for r, slot in zip(rs, slots):
                y = dot(h[:2 * rows, :], ring[slot, :d_model, :])
                for k in range(2):
                    part = y[:, k * head:(k + 1) * head]
                    if r < r_kv:
                        qf[r * 2 + k] = rope(part)
                    elif r == r_kv:
                        kn[k] = rope(part)
                    else:
                        vn[k] = part.astype(BF16).astype(F32)
            for r in rs:
                release(layer, r)

        def chunk_body(ch, carry):
            slot = lax.rem(ch, 2)
            for cp in cache_copies(layer, ch):
                cp.wait()
            for gi in range(CS // GS):
                r0 = al(ch * CS + gi * GS, GS)
                valid = own_keys & (key_pos < len_ref[pl.ds(r0, GS), :])
                for k in range(2):
                    q = qf[k * group:(k + 1) * group, pl.ds(r0, GS), :]
                    keys = kb[slot, gi * GS:(gi + 1) * GS, k].reshape(GS * seq, head)
                    vals = vb[slot, gi * GS:(gi + 1) * GS, k].reshape(GS * seq, head)
                    sc = lax.dot_general(q.reshape(group * GS, head).astype(BF16), keys, (((1,), (1,)), ((), ())),
                                         preferred_element_type=F32)
                    sc = sc.reshape(group, GS, GS * seq) * scale
                    sc = jnp.where(valid[None], sc, -1e30)
                    k_new = kn[k, pl.ds(r0, GS), :]
                    v_new = vn[k, pl.ds(r0, GS), :]
                    self_sc = jnp.sum(q * k_new[None], axis=-1, keepdims=True) * scale
                    top = jnp.maximum(jnp.max(sc, axis=-1, keepdims=True), self_sc)
                    e = jnp.exp(sc - top)
                    self_e = jnp.exp(self_sc - top)
                    total = jnp.sum(e, axis=-1, keepdims=True) + self_e
                    mix = dot(e.reshape(group * GS, GS * seq).astype(BF16), vals).reshape(group, GS, head)
                    mix = mix + self_e.astype(BF16).astype(F32) * v_new[None]
                    of[k * group:(k + 1) * group, gi * GS:(gi + 1) * GS, :] = mix / total
            rr = pl.ds(al(ch * CS, CS), CS)
            for hh in range(heads // 2):
                oa[c, rr, hh * head:(hh + 1) * head] = of[hh].astype(BF16)
            rcopy(oa.at[c, rr], oa.at[c, rr], o_send.at[ch], o_recv.at[ch], pair).start()
            nxt = ch + 2

            @pl.when(nxt < n_chunks)
            def _():
                for cp in cache_copies(layer, nxt):
                    cp.start()

            @pl.when((nxt >= n_chunks) & not_last)
            def _():
                for cp in cache_copies(layer + 1, nxt - n_chunks):
                    cp.start()

            return carry

        n_chunks = 2 * rows // CS
        lax.fori_loop(0, n_chunks, chunk_body, 0)
        for ch in range(n_chunks):
            rr = pl.ds(ch * CS, CS)
            rcopy(oa.at[oc, rr], oa.at[oc, rr], o_send.at[ch], o_recv.at[ch], pair).wait_recv()

        for g0 in range(0, nq, 2):
            js = list(range(g0, min(g0 + 2, nq)))
            slots = [wait_top(layer, r_o + j) for j in js]
            for j, slot in zip(js, slots):
                acc = dot(oa[0], ring[slot, :half_d, :]) + dot(oa[1], ring[slot, half_d:d_model, :])
                acc = acc + xc[c * nq + j].reshape(2 * rows, TN).astype(F32)
                x1[0, c * nq + j] = acc.astype(BF16).reshape(2, rows, TN)
            for j in js:
                mine = c * nq + j
                rcopy(x1.at[0, mine], x1.at[1, mine], xy_send.at[j], xy_recv.at[j], ypeer).start()
                rcopy(x1.at[0, mine], x1.at[0, mine], xp_send.at[j], xp_recv.at[j], pair).start()
                release(layer, r_o + j)
        for j in range(nq):
            theirs = oc * nq + j
            rcopy(x1.at[0, theirs], x1.at[0, theirs], xp_send.at[j], xp_recv.at[j], pair).wait_recv()
        norm_rows(x1, 0, fg_ref, layer, 0)
        for j in range(nq):
            mine = c * nq + j
            rcopy(x1.at[1, mine], x1.at[1, mine], xy_send.at[j], xy_recv.at[j], ypeer).wait_recv()
            rcopy(x1.at[1, mine], x1.at[1, mine], xf_send.at[j], xf_recv.at[j], pair).start()
        for j in range(nq):
            theirs = oc * nq + j
            rcopy(x1.at[1, theirs], x1.at[1, theirs], xf_send.at[j], xf_recv.at[j], pair).wait_recv()
        norm_rows(x1, 1, fg_ref, layer, 2 * rows)

        def gate_up(first, count):
            slots = [wait_top(layer, r_gu + first + i) for i in range(count)]
            for i, slot in enumerate(slots):
                y = dot(h[...], ring[slot, :d_model, :])
                gate = y[:, :128]
                act = gate * (1.0 / (1.0 + jnp.exp(-gate))) * y[:, 128:]
                u[:, pl.ds(al((first + i) * 128, 128), 128)] = act.astype(BF16)
            for i in range(count):
                release(layer, r_gu + first + i)

        full = ngu // GU_UNROLL

        def gu_body(i, carry):
            gate_up(i * GU_UNROLL, GU_UNROLL)
            return carry

        lax.fori_loop(0, full, gu_body, 0)
        if ngu % GU_UNROLL:
            gate_up(full * GU_UNROLL, ngu % GU_UNROLL)

        for j in range(nq):
            mine = c * nq + j
            rcopy(x1.at[1, mine], x1.at[1, mine], xf_send.at[j], xf_recv.at[j], pair).wait_send()

        def pair_sum(j):
            rcopy(yp.at[j, oc], dr.at[j], d_send.at[j], d_recv.at[j], pair).wait_recv()
            yp[j, c, 1] = yp[j, c, 1] + dr[j, 1]
            rcopy(yp.at[j, c, 1], yr.at[j], y_send.at[j], y_recv.at[j], ypeer).start()

        def down_body(i, carry):
            j0 = i * DN_UNROLL
            slots = [wait_full(layer, r_dn + j0 + k) for k in range(DN_UNROLL)]
            for k, slot in enumerate(slots):
                y = dot(u[...], ring[slot])
                for chip in range(2):
                    for core in range(2):
                        r0 = (chip * 2 + core) * rows
                        yp[j0 + k, core, chip] = y[r0:r0 + rows, :]
            for k in range(DN_UNROLL):
                rcopy(yp.at[j0 + k, oc], dr.at[j0 + k], d_send.at[j0 + k], d_recv.at[j0 + k], pair).start()
                release(layer, r_dn + j0 + k)

            @pl.when(i > 0)
            def _():
                for k in range(DN_UNROLL):
                    pair_sum(j0 - DN_UNROLL + k)

            return carry

        lax.fori_loop(0, nch // DN_UNROLL, down_body, 0)
        for k in range(DN_UNROLL):
            pair_sum(nch - DN_UNROLL + k)

        def finish(j, carry):
            rcopy(yp.at[j, c, 1], yr.at[j], y_send.at[j], y_recv.at[j], ypeer).wait_recv()
            y = (yp[j, c, 0] + dr[j, 0] + yr[j]).astype(BF16).astype(F32)
            xc[j, c] = (x1[0, j, c].astype(F32) + y).astype(BF16)

            @pl.when(not_last)
            def _():
                rcopy(xc.at[j, c], xc.at[j, c], e_send.at[j], e_recv.at[j], pair).start()

            @pl.when(jnp.logical_not(not_last))
            def _():
                pltpu.make_async_copy(xc.at[j, c], out.at[:, pl.ds(al(j * TN, TN), TN)], e_send.at[j]).start()

            return carry

        lax.fori_loop(0, nch, finish, 0)

        for ch in range(n_chunks):
            rr = pl.ds(ch * CS, CS)
            rcopy(oa.at[c, rr], oa.at[c, rr], o_send.at[ch], o_recv.at[ch], pair).wait_send()
        for j in range(nq):
            mine = c * nq + j
            rcopy(x1.at[0, mine], x1.at[1, mine], xy_send.at[j], xy_recv.at[j], ypeer).wait_send()
            rcopy(x1.at[0, mine], x1.at[0, mine], xp_send.at[j], xp_recv.at[j], pair).wait_send()
        for j in range(nch):
            rcopy(yp.at[j, oc], dr.at[j], d_send.at[j], d_recv.at[j], pair).wait_send()
            rcopy(yp.at[j, c, 1], yr.at[j], y_send.at[j], y_recv.at[j], ypeer).wait_send()

        @pl.when(not_last)
        def _():
            for j in range(nch):
                rcopy(xc.at[j, oc], xc.at[j, oc], e_send.at[j], e_recv.at[j], pair).wait_recv()
                rcopy(xc.at[j, c], xc.at[j, c], e_send.at[j], e_recv.at[j], pair).wait_send()

        @pl.when(jnp.logical_not(not_last))
        def _():
            for j in range(nch):
                pltpu.make_async_copy(xc.at[j, c], out.at[:, pl.ds(j * TN, TN)], e_send.at[j]).wait()

        return carry

    lax.fori_loop(0, n_layers, layer_body, 0)


def solution(mesh):
    batch_axes = ('inst', 'dev')
    in_specs = (
        P(batch_axes, None),
        P(batch_axes),
        P(None, batch_axes, None, None, None),
        P(None, batch_axes, None, None, None),
        P(), P(), P(), P(), P(),
        P(None, None, 'dev'),
        P(None, None, 'dev'),
        P(None, 'dev', None),
    )
    out_specs = P(('inst', 'dev', 'side'), None)
    n_side = mesh.shape['side']

    def device_fn(hidden, cache_len, k_cache, v_cache, w_q, w_kv, w_o, attn_gain, ffn_gain, w_gate, w_up, w_down):
        n_layers, d_model, _ = w_q.shape
        kv_heads, seq, head = k_cache.shape[2:]
        heads = w_q.shape[2] // head
        rows = hidden.shape[0] // n_side
        ff = w_gate.shape[2] // 2
        nch = d_model // TN
        nq = nch // 2
        side = lax.axis_index('side')
        lengths = lax.dynamic_slice_in_dim(cache_len, (side // 2) * (2 * rows), 2 * rows)
        half_dim = head // 2
        freqs = ROPE_BASE ** (-jnp.arange(half_dim, dtype=F32) / half_dim)
        angle = lengths.astype(F32)[:, None] * jnp.concatenate([freqs, freqs])
        sign = jnp.where(jnp.arange(head) < half_dim, -1.0, 1.0).astype(F32)
        cos_tab = jnp.cos(angle)
        sin_tab = jnp.sin(angle) * sign
        len_tab = jnp.broadcast_to(lengths[:, None], (2 * rows, GS * seq))
        gains = [g.reshape(n_layers, nch, 1, TN) for g in (attn_gain, ffn_gain)]
        dims = (n_layers, d_model, ff, heads, kv_heads, head, seq)
        vmem = pl.BlockSpec(memory_space=pltpu.VMEM)
        hbm = pl.BlockSpec(memory_space=pl.ANY)
        dma = pltpu.SemaphoreType.DMA
        n_chunks = 2 * rows // CS
        return pl.pallas_call(
            functools.partial(kernel, dims),
            name='decode_layers',
            out_shape=jax.ShapeDtypeStruct((rows, d_model), BF16),
            in_specs=[vmem] * 5 + [hbm] * 9,
            out_specs=hbm,
            scratch_shapes=[
                pltpu.VMEM((NS, ff, TN), BF16),
                pltpu.VMEM((nch, 2, rows, TN), BF16),
                pltpu.VMEM((2, nch, 2, rows, TN), BF16),
                pltpu.VMEM((4 * rows, d_model), BF16),
                pltpu.VMEM((heads // 2, 2 * rows, head), F32),
                pltpu.VMEM((2, 2 * rows, head), F32),
                pltpu.VMEM((2, 2 * rows, head), F32),
                pltpu.VMEM((heads // 2, CS, head), F32),
                pltpu.VMEM((2, 2 * rows, d_model // 2), BF16),
                pltpu.VMEM((4 * rows, ff), BF16),
                pltpu.VMEM((nch, 2, 2, rows, TN), F32),
                pltpu.VMEM((nch, 2, rows, TN), F32),
                pltpu.VMEM((nch, rows, TN), F32),
                pltpu.VMEM((2, CS, 2, seq, head), BF16),
                pltpu.VMEM((2, CS, 2, seq, head), BF16),
                dma((NS,)), dma((2, 2)), dma((nch, 2)),
                dma((n_chunks,)), dma((n_chunks,)),
                dma((nq,)), dma((nq,)), dma((nq,)), dma((nq,)), dma((nq,)), dma((nq,)),
                dma((nch,)), dma((nch,)), dma((nch,)), dma((nch,)), dma((nch,)), dma((nch,)),
            ],
            compiler_params=pltpu.CompilerParams(
                collective_id=0, has_side_effects=True, vmem_limit_bytes=67043328),
        )(cos_tab, sin_tab, len_tab, *gains, hidden, k_cache, v_cache, w_q, w_kv, w_o, w_gate, w_up, w_down)

    return jax.shard_map(device_fn, mesh=mesh, in_specs=in_specs, out_specs=out_specs, check_vma=False)
```

time: 1360 us -> 240 us (0.18); the launches traced: 1350 us -> 240 us
  waiting for transfers between devices: 614 us -> 0 us
  local copies, waits for them, and re-layouts: 562 us -> 5.59 us
  Pallas kernels: 0 us -> 233 us
  matrix products: 121 us -> 0 us
  other arithmetic: 25.6 us -> 1.82 us
  between operations: 14 us -> 0.01 us
    reduce_scatter x3 -> x0, waiting for transfers between devices: 412 us -> none  [device_fn(): summed = lax.psum_scatter(part_sum, 'dev', scatter_dimension=0, tiled=True)]
    another operation x9 -> x0, local copies, waits for them, and re-layouts: 361 us -> none
    pallas_call x0 -> x1, Pallas kernels: none -> 233 us  [device_fn(): pl.pallas_call(functools.partial(kernel, dims), name='decode_layers', out...]
    slice x20 -> x0, local copies, waits for them, and re-layouts: 142 us -> none  [the longest x3 62.4 us: attn_branch(): w_q[layer]]
    dot_general x18 -> x0, matrix products: 121 us -> none  [the longest x3 36.3 us: attention_layer(): jnp.dot(normed, q_weight, preferred_element_type=jnp.float32)]
    ppermute x6 -> x0, waiting for transfers between devices: 114 us -> none  [the longest x3 56.4 us: device_fn(): sent = lax.ppermute(x_pair, 'side', to_ffn)]
    all_gather x3 -> x0, waiting for transfers between devices: 87.5 us -> none  [device_fn(): h_all = lax.all_gather(h_rows, 'dev', axis=0, tiled=True)]
    dynamic_slice x6 -> x0, local copies, waits for them, and re-layouts: 36.4 us -> none  [pair_rows(): picked = lax.dynamic_index_in_dim(shaped, slot, axis=1, keepdims=False)]
  transfers between devices with their start and end apart: 12 -> 0, of which waited for: 12 -> 0; matrix products, arithmetic and copies ran while one was open for 0% -> 0% of each run, Pallas kernels for 0% -> 0%
where the time goes in v1:
time: 240 us
  Pallas kernels  233 us (97%)
  local copies, waits for them, and re-layouts  5.59 us (2%)
    pallas_call x1, Pallas kernels, device_fn(): pl.pallas_call(functools.partial(kernel, dims), name='decode_layers', out...  233 us

profile of v1, /device:TPU:0, one launch (start us, length us, event | category | flops | bytes accessed | tf_op | source)
XLA Modules:
  0.0 240.1 jit_solution(13793126694253842227)
XLA Ops:
  0.0 0.1 compare_select_fusion
  0.1 0.8 fusion.1
  0.8 1.5 reshape.14.ag_ref
  2.3 1.5 reshape.15.fg_ref
  3.8 1.0 fusion
  4.8 0.8 broadcast_in_dim.19.len_ref
  5.6 232.7 %decode_layers.1 = bf16[64,3584]{1,0:T(8,128)(2,1)} custom-call(f32[128,128]{1,0:T(8,128)} %get-tuple-element.8.cos_ref, f32[128,128]{1,0:T(8,128)} %get-tuple-element.7.sin_ref, s32[128,512]{1,0:T(8,128)} %broadcast_in_dim.19.len_ref, f32[3,14,1,256]{3,2,1,0:T(1,128)} %reshape.14.ag_ref, f32[3,14,1,256]{3,2,1,0:T(1,128)} %reshape.15.fg_ref, ...), custom_call_target="tpu_custom_call" | custom-call | tf_op jit(solution)/shard_map/decode_layers/pallas_call | solution.py:395
  238.3 1.8 copy.14
  (1 shorter events, 0.0 us)

commit v2 on v0

v2 whole, which is shorter than its diff:
```python
import functools

import jax
import jax.numpy as jnp
import numpy as np
from jax import lax
from jax.experimental import pallas as pl
from jax.experimental.pallas import tpu as pltpu
from jax.sharding import PartitionSpec as P

EPS = 1e-5
ROPE_BASE = 10000.0
MESH = pl.DeviceIdType.MESH
F32 = jnp.float32
BF16 = jnp.bfloat16

TN = 256
NS = 16
GS = 8
GU = 7
DN_STEPS = (2, 2, 2, 2, 2, 2, 2)
QKV_STEPS = (4, 5)
O_STEPS = (2, 2, 3)


def spans(steps, total):
    assert sum(steps) == total
    out, at = [], 0
    for n in steps:
        out.append(list(range(at, at + n)))
        at += n
    return out


def dot(lhs, rhs):
    return jnp.dot(lhs, rhs, preferred_element_type=F32)


def kernel(dims, len_ref, freq_ref, ag_ref, fg_ref, hid, kc, vc, wq, wkv, wo, wg, wu, wd, out,
           ring, xc, x1, h, qf, kn, vn, of, oa, acc_s, u, yp, dr, yr, kb, vb, cos_t, sin_t, len_t,
           ring_sem, cache_sem, in_sem, o_send, o_recv, xp_send, xp_recv, xy_send, xy_recv, xf_send, xf_recv,
           d_send, d_recv, y_send, y_recv, e_send, e_recv):
    n_layers, d_model, ff, heads, kv_heads, head, seq = dims
    half_d = d_model // 2
    nch = d_model // TN
    nq = half_d // TN
    hr = xc.shape[3]
    ngu = ff // 128
    group = heads // kv_heads
    r_o = nq + 2
    r_gu = r_o + nq
    r_dn = r_gu + ngu
    tiles = r_dn + nch
    assert r_gu == NS

    side = lax.axis_index("side")
    dev = lax.axis_index("dev")
    c = lax.rem(side, 2)
    oc = 1 - c
    base = (side - c) * (2 * hr)
    pair = {"side": side + 1 - 2 * c}
    ypeer = {"dev": 1 - dev}

    barrier = pltpu.get_barrier_semaphore()
    pl.semaphore_signal(barrier, inc=1, device_id=pair, device_id_type=MESH)
    pl.semaphore_signal(barrier, inc=1, device_id=ypeer, device_id_type=MESH)

    def rcopy(src, dst, ssem, rsem, where):
        return pltpu.make_async_remote_copy(
            src_ref=src, dst_ref=dst, send_sem=ssem, recv_sem=rsem, device_id=where, device_id_type=MESH)

    def al(v, m):
        return pl.multiple_of(v, m)

    def slot_of(layer, r):
        return lax.rem(layer * tiles + r, NS)

    def fill_attn(layer, r):
        slot = slot_of(layer, r)
        top = ring.at[slot, pl.ds(0, d_model)]
        if r < nq:
            src = wq.at[layer, :, pl.ds(al(c * half_d + r * TN, TN), TN)]
        elif r < r_o:
            src = wkv.at[layer, :, pl.ds(al((r - nq) * (2 * TN) + c * TN, TN), TN)]
        else:
            src = wo.at[layer, :, pl.ds(al(c * half_d + (r - r_o) * TN, TN), TN)]
        pltpu.make_async_copy(src, top, ring_sem.at[slot]).start()

    def fill_gu(layer, i):
        slot = slot_of(layer, r_gu + i)
        col = al(c * ff + i * 128, 128)
        for k, w in enumerate((wg, wu)):
            pltpu.make_async_copy(
                w.at[layer, :, pl.ds(col, 128)], ring.at[slot, pl.ds(0, d_model), pl.ds(k * 128, 128)],
                ring_sem.at[slot]).start()

    def fill_dn(layer, j):
        slot = slot_of(layer, r_dn + j)
        pltpu.make_async_copy(
            wd.at[layer, pl.ds(al(c * ff, 128), ff), pl.ds(al(j * TN, TN), TN)], ring.at[slot], ring_sem.at[slot]).start()

    def wait_top(slot):
        pltpu.make_async_copy(wq.at[0, :, pl.ds(0, TN)], ring.at[slot, pl.ds(0, d_model)], ring_sem.at[slot]).wait()

    def wait_full(slot):
        pltpu.make_async_copy(wd.at[0, pl.ds(0, ff), pl.ds(0, TN)], ring.at[slot], ring_sem.at[slot]).wait()

    def cache_copies(layer, half, core):
        src = pl.ds(al(base + core * (2 * hr) + half * hr, hr), hr)
        hd = pl.ds(c * 2, 2)
        return (pltpu.make_async_copy(kc.at[layer, src, hd], kb.at[core], cache_sem.at[core, 0]),
                pltpu.make_async_copy(vc.at[layer, src, hd], vb.at[core], cache_sem.at[core, 1]))

    def norm_half(read, gain, layer, dst_row):
        for k in range(2):
            total = jnp.zeros((hr, TN), F32)
            for j in range(nch):
                v = read(j, k).astype(F32)
                total = total + v * v
            inv = lax.rsqrt(jnp.sum(total, axis=-1, keepdims=True) * (1.0 / d_model) + EPS)
            r0 = dst_row + k * hr
            for j in range(nch):
                v = read(j, k).astype(F32)
                g = gain[pl.ds(layer, 1), j * TN:(j + 1) * TN]
                h[r0:r0 + hr, j * TN:(j + 1) * TN] = (v * inv * g).astype(BF16)

    def row_copy(j, half, k):
        src = hid.at[pl.ds(al(base + (k * 2 + half) * hr, hr), hr), pl.ds(j * TN, TN)]
        return pltpu.make_async_copy(src, xc.at[j, half, k], in_sem.at[j, half, k])

    rows_in = [[(j, half, k) for j in range(nch) for k in range(2)] for half in range(2)]
    for jhk in rows_in[0]:
        row_copy(*jhk).start()
    for r in range(4):
        fill_attn(0, r)

    n_pos = 4 * hr
    lens = len_ref[pl.ds(lax.div(side, 2), 1), :].astype(F32)
    len_t[...] = jnp.broadcast_to(lens, (n_pos, n_pos)).T
    angle = len_t[:, :head] * freq_ref[...]
    lane = lax.broadcasted_iota(jnp.int32, (n_pos, head), 1)
    cos_t[...] = jnp.cos(angle)
    sin_t[...] = jnp.sin(angle) * jnp.where(lane < head // 2, -1.0, 1.0)

    for jhk in rows_in[0]:
        row_copy(*jhk).wait()
    for r in range(4, r_o):
        fill_attn(0, r)
    for core in range(2):
        for cp in cache_copies(0, 0, core):
            cp.start()
    for jhk in rows_in[1]:
        row_copy(*jhk).start()
    for r in range(r_o, r_gu):
        fill_attn(0, r)
    pl.semaphore_wait(barrier, 2)

    col = lax.broadcasted_iota(jnp.int32, (GS, GS * seq), 1)
    row = lax.broadcasted_iota(jnp.int32, (GS, GS * seq), 0)
    own_keys = lax.shift_right_logical(col, seq.bit_length() - 1) == row
    key_pos = jnp.bitwise_and(col, seq - 1).astype(F32)
    scale = head ** -0.5

    def e_copy(half, j, core):
        return rcopy(xc.at[j, half, core], xc.at[j, half, core], e_send.at[half, j], e_recv.at[half, j], pair)

    def out_copy(half, j):
        dst = out.at[pl.ds(half * hr, hr), pl.ds(al(j * TN, TN), TN)]
        return pltpu.make_async_copy(xc.at[j, half, c], dst, e_send.at[half, j])

    def y_copy(half, j):
        return rcopy(yp.at[j, c, half, 1], yr.at[half, j], y_send.at[half, j], y_recv.at[half, j], ypeer)

    def d_copy(j):
        return rcopy(yp.at[j, oc], dr.at[j], d_send.at[j], d_recv.at[j], pair)

    def finish(half, after):
        def one(j, carry):
            y_copy(half, j).wait_recv()
            y = (yp[j, c, half, 0] + dr[j, half, 0] + yr[half, j]).astype(BF16).astype(F32)
            xc[j, half, c] = (x1[0, j, half, c].astype(F32) + y).astype(BF16)
            after(j)
            return carry

        lax.fori_loop(0, nch, one, 0)

    def exchange(half):
        finish(half, lambda j: e_copy(half, j, c).start())
        for j in range(nch):
            e_copy(half, j, oc).wait_recv()
            e_copy(half, j, c).wait_send()

    def sums_sent():
        for j in range(nch):
            d_copy(j).wait_send()
            for half in range(2):
                y_copy(half, j).wait_send()

    def xy_copy(half, j):
        mine = c * nq + j
        return rcopy(x1.at[0, mine, half], x1.at[1, mine, half], xy_send.at[half, j], xy_recv.at[half, j], ypeer)

    def xp_copy(half, j, core):
        at = x1.at[0, core * nq + j, half]
        return rcopy(at, at, xp_send.at[half, j], xp_recv.at[half, j], pair)

    def xf_copy(half, j, core):
        at = x1.at[1, core * nq + j, half]
        return rcopy(at, at, xf_send.at[half, j], xf_recv.at[half, j], pair)

    def o_copy(half, core, cc):
        at = oa.at[cc, half, pl.ds(al(core * hr, hr), hr)]
        return rcopy(at, at, o_send.at[half, core], o_recv.at[half, core], pair)

    def attention_half(layer, half):
        first = half == 0

        def arrive(rs):
            @pl.when(first)
            def _():
                for r in rs:
                    wait_top(slot_of(layer, r))

        def refill(rs):
            @pl.when(jnp.logical_not(first))
            def _():
                for r in rs:
                    fill_gu(layer, r)

        with jax.named_scope("norm_a"):
            norm_half(lambda j, k: xc[j, half, k], ag_ref, layer, 0)

        def both_cores(table):
            return jnp.concatenate([table[pl.ds(al((k * 2 + half) * hr, hr), hr), :] for k in range(2)], axis=0)

        cos_v = both_cores(cos_t)
        sin_v = both_cores(sin_t)

        def rope(v):
            return (v * cos_v + pltpu.roll(v, head // 2, 1) * sin_v).astype(BF16).astype(F32)

        def qkv(r):
            y = dot(h[:2 * hr, :], ring[slot_of(layer, r), :d_model, :])
            for k in range(2):
                part = y[:, k * head:(k + 1) * head]
                if r < nq:
                    qf[r * 2 + k] = rope(part)
                elif r == nq:
                    kn[k] = rope(part)
                else:
                    vn[k] = part.astype(BF16).astype(F32)

        with jax.named_scope("qkv"):
            for rs in spans(QKV_STEPS, r_o):
                arrive(rs)
                for r in rs:
                    qkv(r)
                refill(rs)

        def core_body(core, carry):
            for cp in cache_copies(layer, half, core):
                cp.wait()
            for gi in range(hr // GS):
                r_tab = al((core * 2 + half) * hr + gi * GS, GS)
                r0 = al(core * hr + gi * GS, GS)
                n_old = len_t[pl.ds(r_tab, GS), :head]
                n_old = jnp.concatenate([n_old] * (GS * seq // head), axis=1)
                valid = own_keys & (key_pos < n_old)
                for k in range(2):
                    q = qf[k * group:(k + 1) * group, pl.ds(r0, GS), :]
                    keys = kb[core, gi * GS:(gi + 1) * GS, k].reshape(GS * seq, head)
                    vals = vb[core, gi * GS:(gi + 1) * GS, k].reshape(GS * seq, head)
                    sc = lax.dot_general(q.reshape(group * GS, head).astype(BF16), keys, (((1,), (1,)), ((), ())),
                                         preferred_element_type=F32)
                    sc = sc.reshape(group, GS, GS * seq) * scale
                    sc = jnp.where(valid[None], sc, -1e30)
                    k_new = kn[k, pl.ds(r0, GS), :]
                    v_new = vn[k, pl.ds(r0, GS), :]
                    self_sc = jnp.sum(q * k_new[None], axis=-1, keepdims=True) * scale
                    top = jnp.maximum(jnp.max(sc, axis=-1, keepdims=True), self_sc)
                    e = jnp.exp(sc - top)
                    self_e = jnp.exp(self_sc - top)
                    total = jnp.sum(e, axis=-1, keepdims=True) + self_e
                    mix = dot(e.reshape(group * GS, GS * seq).astype(BF16), vals).reshape(group, GS, head)
                    mix = mix + self_e.astype(BF16).astype(F32) * v_new[None]
                    of[k * group:(k + 1) * group, gi * GS:(gi + 1) * GS, :] = mix / total
            for hh in range(heads // 2):
                oa[c, half, pl.ds(al(core * hr, hr), hr), hh * head:(hh + 1) * head] = of[hh].astype(BF16)
            o_copy(half, core, c).start()

            @pl.when(first)
            def _():
                for cp in cache_copies(layer, 1, core):
                    cp.start()

            @pl.when(jnp.logical_not(first) & (layer + 1 < n_layers))
            def _():
                for cp in cache_copies(layer + 1, 0, core):
                    cp.start()

            return carry

        with jax.named_scope("attn"):
            lax.fori_loop(0, 2, core_body, 0)

        with jax.named_scope("w_o_own"):
            arrive(range(r_o, r_gu))
            for i in range(nq):
                w = ring[slot_of(layer, r_o + i), pl.ds(al(c * half_d, half_d), half_d), :]
                acc_s[i] = dot(oa[c, half], w) + xc[c * nq + i, half].reshape(2 * hr, TN).astype(F32)
        with jax.named_scope("o_wait"):
            @pl.when(jnp.logical_not(first))
            def _():
                for j in range(nq):
                    xy_copy(0, j).wait_recv()
                    xf_copy(0, j, c).start()

            for core in range(2):
                o_copy(half, core, oc).wait_recv()
        with jax.named_scope("w_o"):
            for js in spans(O_STEPS, nq):
                for i in js:
                    w = ring[slot_of(layer, r_o + i), pl.ds(al(oc * half_d, half_d), half_d), :]
                    acc = acc_s[i] + dot(oa[oc, half], w)
                    x1[0, c * nq + i, half] = acc.astype(BF16).reshape(2, hr, TN)
                for i in js:
                    xy_copy(half, i).start()
                    xp_copy(half, i, c).start()
                refill([r_o + i for i in js])

    def layer_body(layer, carry):
        not_last = layer + 1 < n_layers

        def half_body(half, carry):
            @pl.when((half == 1) & (layer == 0))
            def _():
                for jhk in rows_in[1]:
                    row_copy(*jhk).wait()

            @pl.when((half == 1) & (layer > 0))
            def _():
                with jax.named_scope("finish_b"):
                    exchange(1)
                    sums_sent()

            attention_half(layer, half)
            return carry

        lax.fori_loop(0, 2, half_body, 0)

        with jax.named_scope("ag_wait"):
            for half in range(2):
                for j in range(nq):
                    xp_copy(half, j, oc).wait_recv()
                norm_half(lambda j, k: x1[0, j, half, k], fg_ref, layer, half * 2 * hr)
                if half:
                    for j in range(nq):
                        xy_copy(half, j).wait_recv()
                        xf_copy(half, j, c).start()
                for j in range(nq):
                    xf_copy(half, j, oc).wait_recv()
                norm_half(lambda j, k: x1[1, j, half, k], fg_ref, layer, (2 + half) * 2 * hr)

        def gate_up(first, count, fill):
            slots = [slot_of(layer, r_gu + first + i) for i in range(count)]
            for slot in slots:
                wait_top(slot)
            for i, slot in enumerate(slots):
                y = dot(h[...], ring[slot, :d_model, :])
                gate = y[:, :128]
                act = gate * (1.0 / (1.0 + jnp.exp(-gate))) * y[:, 128:]
                u[:, pl.ds(al((first + i) * 128, 128), 128)] = act.astype(BF16)
            for i in range(count):
                fill(first + i)

        n_a = ngu - NS
        n_b = nch

        def gu_a(i, carry):
            gate_up(i * GU, GU, lambda t: fill_gu(layer, t + NS))
            return carry

        def gu_b(i, carry):
            gate_up(n_a + i * GU, GU, lambda t: fill_dn(layer, t - n_a))
            return carry

        def fill_next(t):
            @pl.when(not_last)
            def _():
                fill_attn(layer + 1, t - n_a - n_b)

        assert n_a % GU == 0 and n_b % GU == 0
        with jax.named_scope("gate_up"):
            lax.fori_loop(0, n_a // GU, gu_a, 0)
            lax.fori_loop(0, n_b // GU, gu_b, 0)
            gate_up(n_a + n_b, ngu - n_a - n_b, fill_next)

        for half in range(2):
            for j in range(nq):
                xf_copy(half, j, c).wait_send()
                xy_copy(half, j).wait_send()
                xp_copy(half, j, c).wait_send()
            for core in range(2):
                o_copy(half, core, c).wait_send()

        def pair_sum(j):
            d_copy(j).wait_recv()
            for half in range(2):
                yp[j, c, half, 1] = yp[j, c, half, 1] + dr[j, half, 1]
            y_copy(0, j).start()

        def down(js, before):
            slots = [slot_of(layer, r_dn + j) for j in js]
            for slot in slots:
                wait_full(slot)
            for j, slot in zip(js, slots):
                y = dot(u[...], ring[slot])
                for chip in range(2):
                    for half in range(2):
                        for core in range(2):
                            r0 = ((chip * 2 + half) * 2 + core) * hr
                            yp[j, core, half, chip] = y[r0:r0 + hr, :]
            for j in js:
                d_copy(j).start()

            @pl.when(not_last)
            def _():
                for j in js:
                    fill_attn(layer + 1, j + ngu - n_a - n_b)

            for j in before:
                pair_sum(j)

        with jax.named_scope("down"):
            steps = spans(DN_STEPS, nch)
            for js, before in zip(steps, [[]] + steps[:-1]):
                down(js, before)
        with jax.named_scope("pair_last"):
            for j in steps[-1]:
                pair_sum(j)
            for j in range(nch):
                y_copy(1, j).start()

        with jax.named_scope("finish_a"):
            @pl.when(not_last)
            def _():
                exchange(0)

            @pl.when(jnp.logical_not(not_last))
            def _():
                finish(0, lambda j: out_copy(0, j).start())

        return carry

    lax.fori_loop(0, n_layers, layer_body, 0)
    with jax.named_scope("finish_b"):
        finish(1, lambda j: out_copy(1, j).start())
        sums_sent()
        for half in range(2):
            for j in range(nch):
                out_copy(half, j).wait()


def solution(mesh):
    batch_axes = ('inst', 'dev')
    in_specs = (
        P(batch_axes, None),
        P(batch_axes),
        P(None, batch_axes, None, None, None),
        P(None, batch_axes, None, None, None),
        P(), P(), P(), P(), P(),
        P(None, None, 'dev'),
        P(None, None, 'dev'),
        P(None, 'dev', None),
    )
    out_specs = P(('inst', 'dev', 'side'), None)
    n_side = mesh.shape['side']

    def device_fn(hidden, cache_len, k_cache, v_cache, w_q, w_kv, w_o, attn_gain, ffn_gain, w_gate, w_up, w_down):
        n_layers, d_model, _ = w_q.shape
        kv_heads, seq, head = k_cache.shape[2:]
        heads = w_q.shape[2] // head
        rows = hidden.shape[0] // n_side
        ff = w_gate.shape[2] // 2
        nch = d_model // TN
        nq = nch // 2
        hr = rows // 2
        half_dim = head // 2
        freqs = np.float32(ROPE_BASE) ** (-np.arange(half_dim, dtype=np.float32) / np.float32(half_dim))
        freqs = jnp.asarray(np.concatenate([freqs, freqs])[None].astype(np.float32))
        lengths = cache_len.reshape(n_side // 2, 2 * rows)
        dims = (n_layers, d_model, ff, heads, kv_heads, head, seq)
        vmem = pl.BlockSpec(memory_space=pltpu.VMEM)
        hbm = pl.BlockSpec(memory_space=pl.ANY)
        dma = pltpu.SemaphoreType.DMA
        return pl.pallas_call(
            functools.partial(kernel, dims),
            name='decode_layers',
            out_shape=jax.ShapeDtypeStruct((rows, d_model), BF16),
            in_specs=[vmem] * 4 + [hbm] * 9,
            out_specs=hbm,
            scratch_shapes=[
                pltpu.VMEM((NS, ff, TN), BF16),
                pltpu.VMEM((nch, 2, 2, hr, TN), BF16),
                pltpu.VMEM((2, nch, 2, 2, hr, TN), BF16),
                pltpu.VMEM((4 * rows, d_model), BF16),
                pltpu.VMEM((heads // 2, rows, head), F32),
                pltpu.VMEM((2, rows, head), F32),
                pltpu.VMEM((2, rows, head), F32),
                pltpu.VMEM((heads // 2, hr, head), F32),
                pltpu.VMEM((2, 2, rows, d_model // 2), BF16),
                pltpu.VMEM((nq, rows, TN), F32),
                pltpu.VMEM((4 * rows, ff), BF16),
                pltpu.VMEM((nch, 2, 2, 2, hr, TN), F32),
                pltpu.VMEM((nch, 2, 2, hr, TN), F32),
                pltpu.VMEM((2, nch, hr, TN), F32),
                pltpu.VMEM((2, hr, 2, seq, head), BF16),
                pltpu.VMEM((2, hr, 2, seq, head), BF16),
                pltpu.VMEM((2 * rows, head), F32),
                pltpu.VMEM((2 * rows, head), F32),
                pltpu.VMEM((2 * rows, 2 * rows), F32),
                dma((NS,)), dma((2, 2)), dma((nch, 2, 2)),
                dma((2, 2)), dma((2, 2)),
                dma((2, nq)), dma((2, nq)), dma((2, nq)), dma((2, nq)), dma((2, nq)), dma((2, nq)),
                dma((nch,)), dma((nch,)), dma((2, nch)), dma((2, nch)), dma((2, nch)), dma((2, nch)),
            ],
            compiler_params=pltpu.CompilerParams(
                collective_id=0, has_side_effects=True, vmem_limit_bytes=67043328),
        )(lengths, freqs, attn_gain, ffn_gain, hidden, k_cache, v_cache, w_q, w_kv, w_o, w_gate, w_up, w_down)

    return jax.shard_map(device_fn, mesh=mesh, in_specs=in_specs, out_specs=out_specs, check_vma=False)
```

time: 1360 us -> 219 us (0.16); the launches traced: 1350 us -> 219 us
  waiting for transfers between devices: 614 us -> 0 us
  local copies, waits for them, and re-layouts: 562 us -> 1.82 us
  Pallas kernels: 0 us -> 217 us
  matrix products: 121 us -> 0 us
  other arithmetic: 25.6 us -> 0 us
  between operations: 14 us -> 0.01 us
    reduce_scatter x3 -> x0, waiting for transfers between devices: 412 us -> none  [device_fn(): summed = lax.psum_scatter(part_sum, 'dev', scatter_dimension=0, tiled=True)]
    another operation x9 -> x0, local copies, waits for them, and re-layouts: 361 us -> none
    pallas_call x0 -> x1, Pallas kernels: none -> 217 us  [device_fn(): pl.pallas_call(functools.partial(kernel, dims), name='decode_layers', out...]
    slice x20 -> x0, local copies, waits for them, and re-layouts: 142 us -> none  [the longest x3 62.4 us: attn_branch(): w_q[layer]]
    dot_general x18 -> x0, matrix products: 121 us -> none  [the longest x3 36.3 us: attention_layer(): jnp.dot(normed, q_weight, preferred_element_type=jnp.float32)]
    ppermute x6 -> x0, waiting for transfers between devices: 114 us -> none  [the longest x3 56.4 us: device_fn(): sent = lax.ppermute(x_pair, 'side', to_ffn)]
    all_gather x3 -> x0, waiting for transfers between devices: 87.5 us -> none  [device_fn(): h_all = lax.all_gather(h_rows, 'dev', axis=0, tiled=True)]
    dynamic_slice x6 -> x0, local copies, waits for them, and re-layouts: 36.4 us -> none  [pair_rows(): picked = lax.dynamic_index_in_dim(shaped, slot, axis=1, keepdims=False)]
  transfers between devices with their start and end apart: 12 -> 0, of which waited for: 12 -> 0; matrix products, arithmetic and copies ran while one was open for 0% -> 0% of each run, Pallas kernels for 0% -> 0%
where the time goes in v2:
time: 219 us
  Pallas kernels  217 us (99%)
    pallas_call x1, Pallas kernels, device_fn(): pl.pallas_call(functools.partial(kernel, dims), name='decode_layers', out...  217 us

profile of v2, /device:TPU:0, one launch (start us, length us, event | category | flops | bytes accessed | tf_op | source)
XLA Modules:
  0.0 218.9 jit_solution(14600467559749610535)
XLA Ops:
  0.0 217.0 %decode_layers.1 = bf16[64,3584]{1,0:T(8,128)(2,1)} custom-call(s32[2,128]{1,0:T(2,128)} %bitcast.1, f32[1,128]{1,0:T(1,128)} %constant.2.clone.freq_ref, f32[3,3584]{1,0:T(4,128)} %ag_ref.1, f32[3,3584]{1,0:T(4,128)} %fg_ref.1, bf16[256,3584]{1,0:T(8,128)(2,1)} %hid.1, bf16[3,256,4,64,128]{4,3,2,1,0:T(8,128)(2,1)} %kc.1, bf16[3,256,4,64,128]{4,3,2,1,0:T(8,128)(2,1)} %vc.1, ...), custom_call_target="tpu_custom_call" | custom-call | tf_op jit(solution)/shard_map/decode_layers/pallas_call | solution.py:496
  217.0 1.8 copy.15

commit v3 on v2

--- a/solution.py
+++ b/solution.py
@@ -37,7 +37,7 @@
 
 
 def kernel(dims, len_ref, freq_ref, ag_ref, fg_ref, hid, kc, vc, wq, wkv, wo, wg, wu, wd, out,
-           ring, xc, x1, h, qf, kn, vn, of, oa, acc_s, u, yp, dr, yr, kb, vb, cos_t, sin_t, len_t,
+           ring, xc, x1, h, qf, kn, vn, p_s, tot_s, self_s, of, oa, acc_s, u, yp, dr, yr, kb, vb, cos_t, sin_t, len_t,
            ring_sem, cache_sem, in_sem, o_send, o_recv, xp_send, xp_recv, xy_send, xy_recv, xf_send, xf_recv,
            d_send, d_recv, y_send, y_recv, e_send, e_recv):
     n_layers, d_model, ff, heads, kv_heads, head, seq = dims
@@ -260,30 +260,40 @@
         def core_body(core, carry):
             for cp in cache_copies(layer, half, core):
                 cp.wait()
-            for gi in range(hr // GS):
-                r_tab = al((core * 2 + half) * hr + gi * GS, GS)
-                r0 = al(core * hr + gi * GS, GS)
-                n_old = len_t[pl.ds(r_tab, GS), :head]
-                n_old = jnp.concatenate([n_old] * (GS * seq // head), axis=1)
-                valid = own_keys & (key_pos < n_old)
-                for k in range(2):
-                    q = qf[k * group:(k + 1) * group, pl.ds(r0, GS), :]
-                    keys = kb[core, gi * GS:(gi + 1) * GS, k].reshape(GS * seq, head)
-                    vals = vb[core, gi * GS:(gi + 1) * GS, k].reshape(GS * seq, head)
-                    sc = lax.dot_general(q.reshape(group * GS, head).astype(BF16), keys, (((1,), (1,)), ((), ())),
-                                         preferred_element_type=F32)
-                    sc = sc.reshape(group, GS, GS * seq) * scale
-                    sc = jnp.where(valid[None], sc, -1e30)
-                    k_new = kn[k, pl.ds(r0, GS), :]
-                    v_new = vn[k, pl.ds(r0, GS), :]
-                    self_sc = jnp.sum(q * k_new[None], axis=-1, keepdims=True) * scale
-                    top = jnp.maximum(jnp.max(sc, axis=-1, keepdims=True), self_sc)
-                    e = jnp.exp(sc - top)
-                    self_e = jnp.exp(self_sc - top)
-                    total = jnp.sum(e, axis=-1, keepdims=True) + self_e
-                    mix = dot(e.reshape(group * GS, GS * seq).astype(BF16), vals).reshape(group, GS, head)
-                    mix = mix + self_e.astype(BF16).astype(F32) * v_new[None]
-                    of[k * group:(k + 1) * group, gi * GS:(gi + 1) * GS, :] = mix / total
+            @pl.when(core >= 0)
+            def _():
+                for gi in range(hr // GS):
+                    n_old = len_t[pl.ds(al((core * 2 + half) * hr + gi * GS, GS), GS), :head]
+                    n_old = jnp.concatenate([n_old] * (GS * seq // head), axis=1)
+                    valid = own_keys & (key_pos < n_old)
+                    r0 = al(core * hr + gi * GS, GS)
+                    for k in range(2):
+                        q = qf[k * group:(k + 1) * group, pl.ds(r0, GS), :]
+                        keys = kb[core, gi * GS:(gi + 1) * GS, k].reshape(GS * seq, head)
+                        sc = lax.dot_general(q.reshape(group * GS, head).astype(BF16), keys, (((1,), (1,)), ((), ())),
+                                             preferred_element_type=F32)
+                        sc = sc.reshape(group, GS, GS * seq) * scale
+                        sc = jnp.where(valid[None], sc, -1e30)
+                        k_new = kn[k, pl.ds(r0, GS), :]
+                        self_sc = jnp.sum(q * k_new[None], axis=-1, keepdims=True) * scale
+                        top = jnp.maximum(jnp.max(sc, axis=-1, keepdims=True), self_sc)
+                        e = jnp.exp(sc - top)
+                        self_e = jnp.exp(self_sc - top)
+                        total = jnp.sum(e, axis=-1, keepdims=True) + self_e
+                        p_s[gi, k] = e.reshape(group * GS, GS * seq).astype(BF16)
+                        tot_s[gi, k] = jnp.broadcast_to(total, (group, GS, head))
+                        self_s[gi, k] = jnp.broadcast_to(self_e, (group, GS, head))
+
+            @pl.when(core >= 0)
+            def _():
+                for gi in range(hr // GS):
+                    r0 = al(core * hr + gi * GS, GS)
+                    for k in range(2):
+                        vals = vb[core, gi * GS:(gi + 1) * GS, k].reshape(GS * seq, head)
+                        mix = dot(p_s[gi, k], vals).reshape(group, GS, head)
+                        mix = mix + self_s[gi, k].astype(BF16).astype(F32) * vn[k, pl.ds(r0, GS), :][None]
+                        of[k * group:(k + 1) * group, gi * GS:(gi + 1) * GS, :] = mix / tot_s[gi, k]
+
             for hh in range(heads // 2):
                 oa[c, half, pl.ds(al(core * hr, hr), hr), hh * head:(hh + 1) * head] = of[hh].astype(BF16)
             o_copy(half, core, c).start()
@@ -485,6 +495,7 @@
         nch = d_model // TN
         nq = nch // 2
         hr = rows // 2
+        group = heads // kv_heads
         half_dim = head // 2
         freqs = np.float32(ROPE_BASE) ** (-np.arange(half_dim, dtype=np.float32) / np.float32(half_dim))
         freqs = jnp.asarray(np.concatenate([freqs, freqs])[None].astype(np.float32))
@@ -507,6 +518,9 @@
                 pltpu.VMEM((heads // 2, rows, head), F32),
                 pltpu.VMEM((2, rows, head), F32),
                 pltpu.VMEM((2, rows, head), F32),
+                pltpu.VMEM((hr // GS, 2, group * GS, GS * seq), BF16),
+                pltpu.VMEM((hr // GS, 2, group, GS, head), F32),
+                pltpu.VMEM((hr // GS, 2, group, GS, head), F32),
                 pltpu.VMEM((heads // 2, hr, head), F32),
                 pltpu.VMEM((2, 2, rows, d_model // 2), BF16),
                 pltpu.VMEM((nq, rows, TN), F32),

time: 219 us -> 204 us (0.932)
  Pallas kernels: 217 us -> 202 us
    pallas_call x1, Pallas kernels: 217 us -> 202 us  [device_fn(): pl.pallas_call(functools.partial(kernel, dims), name='decode_layers', out...]
where the time goes in v3:
time: 204 us
  Pallas kernels  202 us (99%)
    pallas_call x1, Pallas kernels, device_fn(): pl.pallas_call(functools.partial(kernel, dims), name='decode_layers', out...  202 us

profile of v3, /device:TPU:0, one launch (start us, length us, event | category | flops | bytes accessed | tf_op | source)
XLA Modules:
  0.0 203.6 jit_solution(11073452045457747353)
XLA Ops:
  0.0 201.8 %decode_layers.1 = bf16[64,3584]{1,0:T(8,128)(2,1)} custom-call(s32[2,128]{1,0:T(2,128)} %bitcast.1, f32[1,128]{1,0:T(1,128)} %constant.2.clone.freq_ref, f32[3,3584]{1,0:T(4,128)} %ag_ref.1, f32[3,3584]{1,0:T(4,128)} %fg_ref.1, bf16[256,3584]{1,0:T(8,128)(2,1)} %hid.1, bf16[3,256,4,64,128]{4,3,2,1,0:T(8,128)(2,1)} %kc.1, bf16[3,256,4,64,128]{4,3,2,1,0:T(8,128)(2,1)} %vc.1, ...), custom_call_target="tpu_custom_call" | custom-call | tf_op jit(solution)/shard_map/decode_layers/pallas_call | solution.py:507
  201.8 1.8 copy.15

commit v4 on v3

--- a/solution.py
+++ b/solution.py
@@ -18,6 +18,8 @@
 NS = 16
 GS = 8
 GU = 7
+GU_EARLY = 2
+LATE_STEPS = (3, 4, 3, 4)
 DN_STEPS = (2, 2, 2, 2, 2, 2, 2)
 QKV_STEPS = (4, 5)
 O_STEPS = (2, 2, 3)
@@ -358,40 +360,57 @@
 
         lax.fori_loop(0, 2, half_body, 0)
 
-        with jax.named_scope("ag_wait"):
-            for half in range(2):
-                for j in range(nq):
-                    xp_copy(half, j, oc).wait_recv()
-                norm_half(lambda j, k: x1[0, j, half, k], fg_ref, layer, half * 2 * hr)
-                if half:
-                    for j in range(nq):
-                        xy_copy(half, j).wait_recv()
-                        xf_copy(half, j, c).start()
-                for j in range(nq):
-                    xf_copy(half, j, oc).wait_recv()
-                norm_half(lambda j, k: x1[1, j, half, k], fg_ref, layer, (2 + half) * 2 * hr)
-
-        def gate_up(first, count, fill):
+        def norm_f(chip, half):
+            read = lambda j, k: x1[chip, j, half, k]
+            norm_half(read, fg_ref, layer, (chip * 2 + half) * 2 * hr)
+
+        with jax.named_scope("ag_first"):
+            for j in range(nq):
+                xp_copy(0, j, oc).wait_recv()
+            norm_f(0, 0)
+            for j in range(nq):
+                xf_copy(0, j, oc).wait_recv()
+            norm_f(1, 0)
+            for j in range(nq):
+                xp_copy(1, j, oc).wait_recv()
+            norm_f(0, 1)
+
+        def gate_up(first, count, r0, r1, wait, fill):
             slots = [slot_of(layer, r_gu + first + i) for i in range(count)]
-            for slot in slots:
-                wait_top(slot)
+            if wait:
+                for slot in slots:
+                    wait_top(slot)
             for i, slot in enumerate(slots):
-                y = dot(h[...], ring[slot, :d_model, :])
+                y = dot(h[r0:r1, :], ring[slot, :d_model, :])
                 gate = y[:, :128]
                 act = gate * (1.0 / (1.0 + jnp.exp(-gate))) * y[:, 128:]
-                u[:, pl.ds(al((first + i) * 128, 128), 128)] = act.astype(BF16)
-            for i in range(count):
-                fill(first + i)
+                u[r0:r1, pl.ds(al((first + i) * 128, 128), 128)] = act.astype(BF16)
+            if fill:
+                for i in range(count):
+                    fill(first + i)
 
         n_a = ngu - NS
         n_b = nch
-
-        def gu_a(i, carry):
-            gate_up(i * GU, GU, lambda t: fill_gu(layer, t + NS))
+        n_rows = 8 * hr
+        late = 6 * hr
+        assert n_b % GU == 0 and GU_EARLY * GU < NS < n_a
+
+        def gu_early(i, carry):
+            gate_up(i * GU, GU, 0, late, True, None)
+
+            def forward(j, carry):
+                xy_copy(1, j).wait_recv()
+                xf_copy(1, j, c).start()
+                return carry
+
+            lax.fori_loop(nq * i // GU_EARLY, nq * (i + 1) // GU_EARLY, forward, 0)
             return carry
 
+        def fill_a(t):
+            fill_gu(layer, t + NS)
+
         def gu_b(i, carry):
-            gate_up(n_a + i * GU, GU, lambda t: fill_dn(layer, t - n_a))
+            gate_up(n_a + i * GU, GU, 0, n_rows, True, lambda t: fill_dn(layer, t - n_a))
             return carry
 
         def fill_next(t):
@@ -399,11 +418,20 @@
             def _():
                 fill_attn(layer + 1, t - n_a - n_b)
 
-        assert n_a % GU == 0 and n_b % GU == 0
+        with jax.named_scope("gu_early"):
+            lax.fori_loop(0, GU_EARLY, gu_early, 0)
+        with jax.named_scope("ag_last"):
+            for j in range(nq):
+                xf_copy(1, j, oc).wait_recv()
+            norm_f(1, 1)
+        with jax.named_scope("gu_late"):
+            for ts in spans(LATE_STEPS, GU_EARLY * GU):
+                gate_up(ts[0], len(ts), late, n_rows, False, fill_a)
         with jax.named_scope("gate_up"):
-            lax.fori_loop(0, n_a // GU, gu_a, 0)
+            gate_up(GU_EARLY * GU, NS - GU_EARLY * GU, 0, n_rows, True, fill_a)
+            gate_up(NS, n_a - NS, 0, n_rows, True, fill_a)
             lax.fori_loop(0, n_b // GU, gu_b, 0)
-            gate_up(n_a + n_b, ngu - n_a - n_b, fill_next)
+            gate_up(n_a + n_b, ngu - n_a - n_b, 0, n_rows, True, fill_next)
 
         for half in range(2):
             for j in range(nq):

time: 204 us -> 200 us (0.980)
  Pallas kernels: 202 us -> 198 us
    pallas_call x1, Pallas kernels: 202 us -> 198 us  [device_fn(): pl.pallas_call(functools.partial(kernel, dims), name='decode_layers', out...]
where the time goes in v4:
time: 200 us
  Pallas kernels  198 us (99%)
    pallas_call x1, Pallas kernels, device_fn(): pl.pallas_call(functools.partial(kernel, dims), name='decode_layers', out...  198 us

profile of v4, /device:TPU:0, one launch (start us, length us, event | category | flops | bytes accessed | tf_op | source)
XLA Modules:
  0.0 200.0 jit_solution(12274704273482644259)
XLA Ops:
  0.0 198.2 %decode_layers.1 = bf16[64,3584]{1,0:T(8,128)(2,1)} custom-call(s32[2,128]{1,0:T(2,128)} %bitcast.1, f32[1,128]{1,0:T(1,128)} %constant.2.clone.freq_ref, f32[3,3584]{1,0:T(4,128)} %ag_ref.1, f32[3,3584]{1,0:T(4,128)} %fg_ref.1, bf16[256,3584]{1,0:T(8,128)(2,1)} %hid.1, bf16[3,256,4,64,128]{4,3,2,1,0:T(8,128)(2,1)} %kc.1, bf16[3,256,4,64,128]{4,3,2,1,0:T(8,128)(2,1)} %vc.1, ...), custom_call_target="tpu_custom_call" | custom-call | tf_op jit(solution)/shard_map/decode_layers/pallas_call | solution.py:535
  198.2 1.8 copy.15

commit v5 on v4

--- a/solution.py
+++ b/solution.py
@@ -19,7 +19,7 @@
 GS = 8
 GU = 7
 GU_EARLY = 2
-LATE_STEPS = (3, 4, 3, 4)
+LATE_STEPS = (2, 3, 3, 3, 3)
 DN_STEPS = (2, 2, 2, 2, 2, 2, 2)
 QKV_STEPS = (4, 5)
 O_STEPS = (2, 2, 3)
@@ -161,6 +161,7 @@
     row = lax.broadcasted_iota(jnp.int32, (GS, GS * seq), 0)
     own_keys = lax.shift_right_logical(col, seq.bit_length() - 1) == row
     key_pos = jnp.bitwise_and(col, seq - 1).astype(F32)
+    masked = jnp.where(own_keys, -1e30, -jnp.inf)
     scale = head ** -0.5
 
     def e_copy(half, j, core):
@@ -275,7 +276,7 @@
                         sc = lax.dot_general(q.reshape(group * GS, head).astype(BF16), keys, (((1,), (1,)), ((), ())),
                                              preferred_element_type=F32)
                         sc = sc.reshape(group, GS, GS * seq) * scale
-                        sc = jnp.where(valid[None], sc, -1e30)
+                        sc = jnp.where(valid[None], sc, masked[None])
                         k_new = kn[k, pl.ds(r0, GS), :]
                         self_sc = jnp.sum(q * k_new[None], axis=-1, keepdims=True) * scale
                         top = jnp.maximum(jnp.max(sc, axis=-1, keepdims=True), self_sc)

time: 200 us -> 200 us (level)
  no operation moved by 1% of the time
where the time goes in v5:
time: 200 us
  Pallas kernels  198 us (99%)
    pallas_call x1, Pallas kernels, device_fn(): pl.pallas_call(functools.partial(kernel, dims), name='decode_layers', out...  198 us

profile of v5, /device:TPU:0, one launch (start us, length us, event | category | flops | bytes accessed | tf_op | source)
XLA Modules:
  0.0 199.8 jit_solution(17824515870113269588)
XLA Ops:
  0.0 198.0 %decode_layers.1 = bf16[64,3584]{1,0:T(8,128)(2,1)} custom-call(s32[2,128]{1,0:T(2,128)} %bitcast.1, f32[1,128]{1,0:T(1,128)} %constant.2.clone.freq_ref, f32[3,3584]{1,0:T(4,128)} %ag_ref.1, f32[3,3584]{1,0:T(4,128)} %fg_ref.1, bf16[256,3584]{1,0:T(8,128)(2,1)} %hid.1, bf16[3,256,4,64,128]{4,3,2,1,0:T(8,128)(2,1)} %kc.1, bf16[3,256,4,64,128]{4,3,2,1,0:T(8,128)(2,1)} %vc.1, ...), custom_call_target="tpu_custom_call" | custom-call | tf_op jit(solution)/shard_map/decode_layers/pallas_call | solution.py:536
  198.0 1.8 copy.15
